TPU v7x, 32 devices: a whole 2x2x4 slice. The times are simulated.
32 devices in a mesh: xz: 16 (over z, y, x), gy: 2 (over core).
Axes of the slice: x: 2, y: 2, z: 4, core: 2. Of those that a mesh axis runs over, the one named last changes fastest.
Arguments:
- initial_state: float32 [3, 2, 16, 512, 512], P(None, None, 'gy', 'xz'), may hold values from -6 to 6
- drag_rate: float32 [16, 512, 1024], P('gy', 'xz'), may hold values from 0.02 to 0.6
- wall_control: float32 [512, 1024], P('xz'), may hold values from -6 to 6
- lift_profile: float32 [16], replicated, may hold values from 0.05 to 0.3
- schur_inverse: float32 [16, 8, 512, 512], P('gy', None, 'xz'), may hold values from -1 to 3, as said below
Outputs:
- final_state: float32 [3, 2, 16, 512, 512], P(None, None, 'gy', 'xz')
- control_gradient: float32 [512, 1024], P('xz', 'gy')
Inputs may be any that keep to these rules, and one draw needn't show every extreme that they name: `schur_inverse`: each 8 x 8 block of one wavenumber holds the precomputed inverse of a Schur complement; dimension 1 indexes the block's columns.
All inputs are finite; a program needn't handle non-finite values.
Results may differ from a plain program's by a relative error of at most 0.00014.
Values sent between devices are 32-bit elements; how exact they have to be, the bound alone decides.
A program may use at most 128 MiB of HBM per device.

v0:
```python
import functools
import math

import jax
import jax.numpy as jnp
import ml_dtypes
import numpy as np
from jax import lax
from jax.experimental import pallas as pl
from jax.experimental.pallas import tpu as pltpu
from jax.sharding import PartitionSpec as P

STEPS = 2


DIFFUSION = 0.04
HIGHEST = lax.Precision.HIGHEST
MESH = pl.DeviceIdType.MESH
LANES = 128
QUAD = 4
HALVES = 2
SUBLANES = 8


def split_host(table):
    high = table.astype(ml_dtypes.bfloat16)
    low = (table - high.astype(np.float64)).astype(ml_dtypes.bfloat16)
    return np.stack([high, low])


def host_tables(stream_len, span_count, count):
    z = np.arange(span_count)
    angle = 2.0 * math.pi / span_count * (np.outer(z, z) % span_count)
    span = np.concatenate([np.cos(angle), np.sin(angle)], axis=1) / math.sqrt(span_count)
    n = np.arange(stream_len)
    k = np.arange(stream_len // 2)
    angle = 2.0 * math.pi / stream_len * (np.outer(k, n) % stream_len)
    stream = np.stack([np.cos(angle), -np.sin(angle)]) / math.sqrt(stream_len)
    stream = stream.reshape(2, count, HALVES, -1, stream_len).transpose(2, 1, 0, 3, 4).reshape(-1, stream_len)
    return split_host(span), split_host(stream.T.copy()), split_host(stream)


def split_pair(x):
    high = x.astype(jnp.bfloat16)
    low = (x - high.astype(jnp.float32)).astype(jnp.bfloat16)
    return high, low


def mxu(a, b):
    return jnp.dot(a, b, preferred_element_type=jnp.float32)


def span_product(x, table):
    high, low = split_pair(x)
    both = mxu(jnp.concatenate([high, low], axis=0), table[0])
    return both[: x.shape[0]] + (both[x.shape[0] :] + mxu(high, table[1]))


def stream_product(table, pair, store):
    tile = table.shape[1] // HALVES

    def body(index, carry):
        rows = pl.ds(pl.multiple_of(index * tile, tile), tile)
        wide = mxu(table[0, rows, :], pair[...])
        narrow = mxu(table[1, rows, :], pair[:, :LANES])
        store(index, rows, wide[:, :LANES] + (wide[:, LANES:] + narrow))
        return carry

    lax.fori_loop(0, HALVES, body, 0)


def fill_pair(pair, rows, x):
    high, low = split_pair(x)
    pair[rows, :LANES] = high
    pair[rows, LANES:] = low


def swap_groups(tiles):
    a0, a1, a2, a3 = tiles
    group = lax.broadcasted_iota(jnp.int32, a0.shape, a0.ndim - 1) // (LANES // QUAD)
    lower = group < 2
    even = group % 2 == 0
    axis = a0.ndim - 1
    half = LANES // 2
    step = LANES // QUAD

    def far(x, y):
        return (
            jnp.where(lower, x, pltpu.roll(y, half, axis)),
            jnp.where(lower, pltpu.roll(x, half, axis), y),
        )

    def near(x, y):
        return (
            jnp.where(even, x, pltpu.roll(y, step, axis)),
            jnp.where(even, pltpu.roll(x, LANES - step, axis), y),
        )

    b0, b2 = far(a0, a2)
    b1, b3 = far(a1, a3)
    return near(b0, b1) + near(b2, b3)


def peer_at(count, me, step):
    peer = 0
    unit = 1
    while unit < count:
        peer = peer + lax.rem(lax.div(me, unit) + lax.div(step, unit), 2) * unit
        unit *= 2
    return peer


class Exchange:
    def __init__(self, count, me, outbox, inbox, send_sem, recv_sem):
        self.count, self.me = count, me
        self.outbox, self.inbox, self.send_sem, self.recv_sem = outbox, inbox, send_sem, recv_sem

    def copy(self, peer, slot):
        return pltpu.make_async_remote_copy(
            src_ref=self.outbox.at[peer],
            dst_ref=self.inbox.at[slot],
            send_sem=self.send_sem.at[peer],
            recv_sem=self.recv_sem.at[slot],
            device_id={"xz": peer},
            device_id_type=MESH,
        )

    def loop(self, action):
        def body(step, carry):
            action(peer_at(self.count, self.me, step))
            return carry

        lax.fori_loop(1, self.count, body, 0)

    def start(self):
        self.loop(lambda peer: self.copy(peer, self.me).start())
        self.inbox[self.me] = self.outbox[self.me]

    def arrive(self):
        self.loop(lambda peer: self.copy(peer, peer).wait_recv())

    def finish(self):
        self.loop(lambda peer: self.copy(peer, peer).wait_send())


def fused_kernel(count, stream_len, *refs):
    refs = list(refs)
    lift, state_far, drag_far, control_far, schur_far, span_far, inverse_far, forward_far = refs[:8]
    final_far, gradient = refs[8:10]
    (
        fields, final, base, source, drag_term, direct, schur, drag_raw, drag, control, control_hat,
        span, inverse, forward, out1, in1, out2, in2, pair, damped, outc, inc, outp, inp,
        halo_u, halo_v, halo_w, halo_final, rim, corner, wall, share, share_in,
        load_sem, send_sem, recv_sem, plane_send, plane_recv, near_send, near_recv, store_sem,
    ) = refs[10:]
    me = lax.axis_index("xz")
    slab = lax.axis_index("gy")
    rows, width, span_count = fields.shape[2], fields.shape[4], fields.shape[5]
    modes = HALVES * width
    chunks = rows // QUAD
    groups = count // QUAD
    tiles_q = span_count // LANES
    tiles = width // SUBLANES * tiles_q
    block = rows * width
    edge = (rows - 1) * (1 - slab)
    has_above = slab.astype(jnp.float32)
    has_below = 1.0 - has_above

    loads = {
        "stream": (state_far.at[0], fields.at[0]),
        "span": (span_far, span),
        "forward": (forward_far, forward),
        "control": (control_far, control),
        "inverse": (inverse_far, inverse),
        "drag": (drag_far, drag_raw),
        "rest": (state_far.at[1:3], fields.at[1:3]),
        "schur": (schur_far, schur),
    }
    loads = {
        name: pltpu.make_async_copy(far, near, load_sem.at[i]) for i, (name, (far, near)) in enumerate(loads.items())
    }
    for load in loads.values():
        load.start()

    barrier = pltpu.get_barrier_semaphore()

    def greet(step, carry):
        pl.semaphore_signal(barrier, inc=1, device_id={"xz": peer_at(count, me, step)}, device_id_type=MESH)
        return carry

    lax.fori_loop(1, count, greet, 0)
    pl.semaphore_signal(barrier, inc=1, device_id={"gy": 1 - slab}, device_id_type=MESH)
    pl.semaphore_wait(barrier, count)

    def first(h, g):
        return Exchange(count, me, out1.at[h, g], in1.at[h, g], send_sem.at[0, h, g], recv_sem.at[0, h, g])

    def second(h, g):
        return Exchange(count, me, out2.at[h, g], in2.at[h, g], send_sem.at[1, h, g], recv_sem.at[1, h, g])

    def across(src, dst, index):
        return pltpu.make_async_remote_copy(
            src_ref=src,
            dst_ref=dst,
            send_sem=near_send.at[index],
            recv_sem=near_recv.at[index],
            device_id={"gy": 1 - slab},
            device_id_type=MESH,
        )

    def halo_copies(h):
        pair_row = (rows - 2) * (1 - slab)
        return [
            across(fields.at[0, :, edge, h], halo_u.at[h], h),
            across(fields.at[1, :, pl.ds(pair_row, 2), h], halo_v.at[h], HALVES + h),
            across(fields.at[2, :, edge, h], halo_w.at[h], 2 * HALVES + h),
        ]

    def rim_copy(h):
        return across(direct.at[:, edge], rim.at[h], 3 * HALVES + h)

    def final_copy(h):
        return across(final.at[1, :, edge, h], halo_final.at[h], 4 * HALVES + h)

    corner_copy = across(schur.at[edge, edge], corner, 5 * HALVES)
    share_copy = across(share.at[1 - slab], share_in, 5 * HALVES + 1)

    def store_copy(h):
        return pltpu.make_async_copy(final.at[:, :, :, h], final_far.at[:, :, :, h], store_sem.at[h])

    def every_half(action):
        def body(h, carry):
            action(h)
            return carry

        lax.fori_loop(0, HALVES, body, 0)

    def every_tile(action):
        def body(t, carry):
            sub = lax.div(t, tiles_q)
            column = lax.rem(t, tiles_q)
            at = (
                pl.ds(pl.multiple_of(sub * SUBLANES, SUBLANES), SUBLANES),
                pl.ds(pl.multiple_of(column * LANES, LANES), LANES),
            )
            action(at, sub, column)
            return carry

        lax.fori_loop(0, tiles, body, 0)

    def mode_ids(h, sub):
        return me * modes + h * width + sub * SUBLANES + lax.broadcasted_iota(jnp.int32, (SUBLANES, LANES), 0)

    def waves(h, sub, column):
        kx = 2.0 * math.pi / stream_len * mode_ids(h, sub).astype(jnp.float32)
        q = column * LANES + lax.broadcasted_iota(jnp.int32, (SUBLANES, LANES), 1)
        signed = jnp.where(q < span_count // 2, q, q - span_count)
        kz = jnp.where(q == span_count // 2, 0.0, 2.0 * math.pi / span_count * signed.astype(jnp.float32))
        return kx, kz

    def mode_weight(h, sub):
        return jnp.where(mode_ids(h, sub) == 0, 1.0, 2.0)

    def send_first(h, weighted):
        x = fields[0, :, :, h]
        if weighted:
            ids = me * modes + h * width + lax.broadcasted_iota(jnp.int32, x.shape, 2)
            x = x * jnp.where(ids == 0, 1.0, 2.0)
        w = span_product(x.reshape(2 * block, span_count), span)
        halfway = (
            w[:block, :span_count] - w[block:, span_count:],
            w[:block, span_count:] + w[block:, :span_count],
        )
        for g in range(chunks):
            for part in range(2):
                for group in range(groups):
                    lanes = slice(LANES * group, LANES * (group + 1))
                    start = width * QUAD * g
                    parts = [halfway[part][start + width * y : start + width * (y + 1), lanes] for y in range(QUAD)]
                    for i, tile in enumerate(swap_groups(parts)):
                        out1[h, g, QUAD * group + i, part] = tile
            first(h, g).start()

    def physical(again):
        for g in range(chunks):
            for h in range(HALVES):
                first(h, g).arrive()
                fill_pair(pair, slice(h * block * 4, (h + 1) * block * 4), in1[h, g].reshape(-1, LANES))
                if again:
                    second(h, g).finish()

            def damp(index, at, y):
                fill_pair(damped, at, y * drag[g, at, :])

            stream_product(inverse, pair, damp)

            def keep(index, at, y):
                out2[index, g] = y.reshape(count, 2, width, LANES)

            stream_product(forward, damped, keep)
            second(0, g).start()
        for h in range(1, HALVES):
            for g in range(chunks):
                second(h, g).start()

    def collect(h):
        for g in range(chunks):
            second(h, g).arrive()
            first(h, g).finish()
        parts = []
        for part in range(2):
            for g in range(chunks):
                columns = []
                for group in range(groups):
                    pieces = [in2[h, g, QUAD * group + i, part] for i in range(QUAD)]
                    columns.append(jnp.concatenate(swap_groups(pieces), axis=0))
                parts.append(jnp.concatenate(columns, axis=1))
        w = span_product(jnp.concatenate(parts, axis=0), span)
        shape = (rows, width, span_count)
        drag_term[0] = (w[:block, :span_count] + w[block:, span_count:]).reshape(shape)
        drag_term[1] = (w[block:, :span_count] - w[:block, span_count:]).reshape(shape)

    def spread(h, forced):
        def body(at, sub, column):
            kx, kz = waves(h, sub, column)
            keep = 1.0 - DIFFUSION * (2.0 + kx * kx + kz * kz)

            def smooth(lines):
                return [
                    lines[i] * keep + DIFFUSION * (lines[i - 1] + lines[i + 1]) for i in range(1, len(lines) - 1)
                ]

            def wide(halo, c, p):
                line = halo[(h, p) + at]
                return [has_above * line] + [fields[(c, p, y, h) + at] for y in range(rows)] + [has_below * line]

            stream = [smooth(wide(halo_u, 0, p)) for p in range(2)]
            across_span = [smooth(wide(halo_w, 2, p)) for p in range(2)]
            for p in range(2):
                outer, inner = halo_v[(h, p, 0) + at], halo_v[(h, p, 1) + at]
                lines = [has_above * outer, has_above * inner]
                lines += [fields[(1, p, y, h) + at] for y in range(rows)]
                lines += [has_below * outer, has_below * inner]
                lines = smooth(lines)
                if forced:
                    hat = control_hat[(p, h) + at]
                    places = [slab * (rows - 1)] + [slab * rows + y for y in range(rows)] + [rows]
                    lines = [line + lift[place] * hat for line, place in zip(lines, places)]
                lines = [has_above * lines[0]] + lines[1:-1] + [has_below * lines[-1]]
                sign = -1.0 if p == 0 else 1.0
                for y in range(rows):
                    base[(0, p, y, h) + at] = stream[p][y]
                    base[(1, p, y, h) + at] = lines[y + 1]
                    base[(2, p, y, h) + at] = across_span[p][y]
                    turned = sign * (kx * stream[1 - p][y] + kz * across_span[1 - p][y])
                    source[(p, y, h) + at] = turned + 0.5 * (lines[y + 2] - lines[y])

        every_tile(body)

    def apply_blocks(h, at, values, transposed):
        for i in range(rows):
            totals = [None, None]
            for j in range(rows):
                place = (j, i) if transposed else (i, j)
                factor = schur[place + (h,) + at]
                for p in range(2):
                    term = factor * values[p][j]
                    totals[p] = term if totals[p] is None else totals[p] + term
            for p in range(2):
                direct[(p, i) + at] = totals[p]

    def begin_solve(h, transposed):
        def body(at, sub, column):
            kx, _ = waves(h, sub, column)
            if transposed:
                kx = kx * mode_weight(h, sub)
            values = [
                [source[(0, y, h) + at] + kx * drag_term[(1, y) + at] for y in range(rows)],
                [source[(1, y, h) + at] - kx * drag_term[(0, y) + at] for y in range(rows)],
            ]
            apply_blocks(h, at, values, transposed)

        every_tile(body)

    def begin_adjoint(h):
        def body(at, sub, column):
            kx, kz = waves(h, sub, column)
            values = []
            for p in range(2):
                line = halo_final[(h, p) + at]
                lines = [has_above * line] + [final[(1, p, y, h) + at] for y in range(rows)] + [has_below * line]
                sign = -1.0 if p == 0 else 1.0
                values.append(
                    [
                        sign * (kx * final[(0, 1 - p, y, h) + at] + kz * final[(2, 1 - p, y, h) + at])
                        + 0.5 * (lines[y + 2] - lines[y])
                        for y in range(rows)
                    ]
                )
            apply_blocks(h, at, values, True)

        every_tile(body)

    def swap_rims(h):
        copy = rim_copy(h)
        copy.start()
        copy.wait_recv()
        copy.wait_send()

    def pressure_at(h, at, transposed):
        turn = corner[(h,) + at]
        reach = [schur[((edge, i) if transposed else (i, edge)) + (h,) + at] for i in range(rows)]
        own = schur[(edge, edge, h) + at]
        wide = []
        for p in range(2):
            near = direct[(p, edge) + at]
            far = rim[(h, p) + at]
            outer = far + has_below * (turn * near)
            above = has_above * (far + turn * (near + own * far))
            inside = [direct[(p, y) + at] + reach[y] * outer for y in range(rows)]
            wide.append([above] + inside + [has_below * outer])
        return wide

    def finish_solve(h, target):
        def body(at, sub, column):
            kx, kz = waves(h, sub, column)
            wide = pressure_at(h, at, False)
            for p in range(2):
                sign = 1.0 if p == 0 else -1.0
                for y in range(rows):
                    turned = sign * wide[1 - p][y + 1]
                    slope = 0.5 * (wide[p][y + 2] - wide[p][y])
                    target[(0, p, y, h) + at] = base[(0, p, y, h) + at] - drag_term[(p, y) + at] + kx * turned
                    target[(1, p, y, h) + at] = base[(1, p, y, h) + at] - slope
                    target[(2, p, y, h) + at] = base[(2, p, y, h) + at] + kz * turned

        every_tile(body)

    def finish_adjoint(h, last):
        def body(at, sub, column):
            kx, kz = waves(h, sub, column)
            wide = pressure_at(h, at, True)
            for p in range(2):
                sign = 1.0 if p == 0 else -1.0
                total = None
                for y in range(rows):
                    slope = 0.5 * (wide[p][y + 2] - wide[p][y])
                    if last:
                        normal = base[(1, p, y, h) + at] - slope
                    else:
                        turned = sign * wide[1 - p][y + 1]
                        normal = final[(1, p, y, h) + at] - slope
                        fields[(0, p, y, h) + at] = final[(0, p, y, h) + at] + kx * turned
                        fields[(1, p, y, h) + at] = normal
                        fields[(2, p, y, h) + at] = final[(2, p, y, h) + at] + kz * turned
                    term = lift[slab * rows + y] * normal
                    total = term if total is None else total + term
                wall[(p, h) + at] = wall[(p, h) + at] + total if last else total

        every_tile(body)

    def start_halos(h):
        for copy in halo_copies(h):
            copy.start()

    def spread_all(forced):
        def body(h):
            for copy in halo_copies(h):
                copy.wait_recv()
                copy.wait_send()
            spread(h, forced)

        every_half(body)

    loads["stream"].wait()
    loads["span"].wait()
    every_half(lambda h: send_first(h, True))

    loads["control"].wait()
    loads["forward"].wait()
    third = Exchange(count, me, outc, inc, plane_send.at[0], plane_recv.at[0])
    lines = control[...]
    blank = jnp.zeros((LANES - lines.shape[0], stream_len), jnp.float32)
    fill_pair(pair, slice(None), jnp.concatenate([lines, blank], axis=0).T)

    def pack(index, at, y):
        y = y.reshape(count, 2, HALVES, SUBLANES, LANES)
        damped_rows = y[:, :, 0] + pltpu.roll(y[:, :, 1], LANES // QUAD, 3)

        @pl.when(index == 0)
        def _():
            outc[...] = damped_rows

        @pl.when(index != 0)
        def _():
            outc[...] = outc[...] + pltpu.roll(damped_rows, LANES // 2, 3)

    stream_product(forward, pair, pack)
    third.start()
    loads["rest"].wait()
    every_half(start_halos)
    loads["schur"].wait()
    corner_copy.start()
    loads["drag"].wait()
    for g in range(chunks):
        drag[g] = drag_raw[QUAD * g : QUAD * (g + 1)].reshape(LANES, stream_len).T
    loads["inverse"].wait()
    physical(False)
    third.arrive()
    parts = []
    for part in range(2):
        columns = []
        for group in range(groups):
            pieces = [inc[QUAD * group + i, part] for i in range(QUAD)]
            columns.append(jnp.concatenate(swap_groups(pieces), axis=0))
        parts.append(jnp.concatenate(columns, axis=1))
    w = span_product(jnp.concatenate(parts, axis=0), span)
    shape = (HALVES, width, span_count)
    control_hat[0] = (w[:modes, :span_count] + w[modes:, span_count:]).reshape(shape)
    control_hat[1] = (w[modes:, :span_count] - w[:modes, span_count:]).reshape(shape)
    corner_copy.wait_recv()
    corner_copy.wait_send()
    spread_all(True)

    def step(h):
        collect(h)
        begin_solve(h, False)
        swap_rims(h)
        finish_solve(h, fields)
        send_first(h, True)
        start_halos(h)

    every_half(step)
    physical(True)
    spread_all(True)

    def turn(h):
        collect(h)
        begin_solve(h, False)
        swap_rims(h)
        finish_solve(h, final)
        copy = final_copy(h)
        copy.start()
        store_copy(h).start()
        copy.wait_recv()
        copy.wait_send()
        begin_adjoint(h)
        swap_rims(h)
        finish_adjoint(h, False)
        send_first(h, False)
        start_halos(h)

    every_half(turn)
    physical(True)
    spread_all(False)

    def close(h):
        collect(h)
        begin_solve(h, True)
        swap_rims(h)
        finish_adjoint(h, True)

    every_half(close)
    fourth = Exchange(count, me, outp, inp, plane_send.at[1], plane_recv.at[1])
    w = span_product(wall[...].reshape(2 * modes, span_count), span)
    halfway = (
        w[:modes, :span_count] - w[modes:, span_count:],
        w[:modes, span_count:] + w[modes:, :span_count],
    )
    for part in range(2):
        for group in range(groups):
            lanes = slice(LANES * group, LANES * (group + 1))
            pieces = [halfway[part][SUBLANES * j : SUBLANES * (j + 1), lanes] for j in range(QUAD)]
            for i, tile in enumerate(swap_groups(pieces)):
                outp[QUAD * group + i, part] = tile
    fourth.start()
    fourth.arrive()
    x = inp[...]
    turned = [x] + [pltpu.roll(x, LANES - j * LANES // QUAD, 3) for j in range(1, QUAD)]
    for h in range(HALVES):
        both = jnp.concatenate(turned[2 * h : 2 * h + 2], axis=2)
        fill_pair(pair, slice(h * block * 4, (h + 1) * block * 4), both.reshape(-1, LANES))

    def keep_share(index, at, y):
        share[index] = y.T[: share.shape[1]]

    stream_product(inverse, pair, keep_share)
    share_copy.start()
    third.finish()
    fourth.finish()
    for h in range(HALVES):
        store_copy(h).wait()
        for g in range(chunks):
            second(h, g).finish()
    share_copy.wait_recv()
    share_copy.wait_send()
    gradient[...] = share[slab] + share_in[...]


VMEM = pl.BlockSpec(memory_space=pltpu.VMEM)
SMEM = pl.BlockSpec(memory_space=pltpu.SMEM)
FAR = pl.BlockSpec(memory_space=pl.ANY)


def fused_call(count, initial_state, drag_rate, wall_control, lift_profile, schur_inverse):
    _, _, rows, modes, span_count = initial_state.shape
    stream_len = drag_rate.shape[2]
    narrow = wall_control.shape[0]
    width = modes // HALVES
    chunks = rows // QUAD
    span, inverse, forward = host_tables(stream_len, span_count, count)
    state = initial_state.reshape(3, 2, rows, HALVES, width, span_count)
    schur = schur_inverse.reshape(rows, rows, HALVES, width, span_count)
    plane = (2, rows, HALVES, width, span_count)
    half_plane = (2, rows, width, span_count)
    box = (HALVES, chunks, count, 2, width, LANES)
    thin = (count, 2, SUBLANES, LANES)
    line = (HALVES, 2, width, span_count)

    def buffer(*shape):
        return pltpu.VMEM(shape, jnp.float32)

    pairs = pltpu.VMEM((stream_len, 2 * LANES), jnp.bfloat16)
    scratch = [buffer(*state.shape)] * 3 + [buffer(*plane), buffer(*half_plane), buffer(*half_plane)]
    scratch += [buffer(*schur.shape), buffer(*drag_rate.shape), buffer(chunks, stream_len, LANES)]
    scratch += [buffer(*wall_control.shape), buffer(*line)]
    scratch += [pltpu.VMEM(table.shape, jnp.bfloat16) for table in (span, inverse, forward)]
    scratch += [buffer(*box)] * 4 + [pairs] * 2 + [buffer(*thin)] * 4
    scratch += [buffer(*line), buffer(HALVES, 2, 2, width, span_count), buffer(*line), buffer(*line), buffer(*line)]
    scratch += [buffer(HALVES, width, span_count), buffer(*line)]
    scratch += [buffer(2, narrow, stream_len // 2), buffer(narrow, stream_len // 2)]
    scratch += [pltpu.SemaphoreType.DMA((8,))]
    scratch += [pltpu.SemaphoreType.DMA((2, HALVES, chunks, count))] * 2
    scratch += [pltpu.SemaphoreType.DMA((2, count))] * 2
    scratch += [pltpu.SemaphoreType.DMA((5 * HALVES + 2,))] * 2
    scratch += [pltpu.SemaphoreType.DMA((HALVES,))]
    final, gradient = pl.pallas_call(
        functools.partial(fused_kernel, count, stream_len),
        out_shape=[
            jax.ShapeDtypeStruct(state.shape, jnp.float32),
            jax.ShapeDtypeStruct((narrow, stream_len // 2), jnp.float32),
        ],
        in_specs=[SMEM] + [FAR] * 7,
        out_specs=[FAR, VMEM],
        scratch_shapes=scratch,
        compiler_params=pltpu.CompilerParams(
            collective_id=0, has_side_effects=True, vmem_limit_bytes=63 * 1024 * 1024
        ),
        cost_estimate=pl.CostEstimate(flops=60_000_000_000, bytes_accessed=32_000_000, transcendentals=0),
    )(lift_profile, state, drag_rate, wall_control, schur, span, inverse, forward)
    return final.reshape(initial_state.shape), gradient


def phase_pair(outer_size, inner_size, period, factor):
    outer_ids = jnp.arange(outer_size, dtype=jnp.int32)[:, None]
    inner_ids = jnp.arange(inner_size, dtype=jnp.int32)[None, :]
    angle = 2.0 * math.pi / period * (outer_ids * inner_ids % period).astype(jnp.float32)
    return (jnp.cos(angle) * factor, jnp.sin(angle) * factor)


def plain_transforms(count, rows, modes, span_count, stream_len):
    half_len = stream_len // 2
    cos_x, sin_x = phase_pair(stream_len, half_len, stream_len, 1.0 / math.sqrt(stream_len))
    cos_z, sin_z = phase_pair(span_count, span_count, span_count, 1.0 / math.sqrt(span_count))

    def to_spectral(physical):
        real_half = jnp.einsum("yzn,nk->yzk", physical, cos_x, precision=HIGHEST)
        imag_half = -jnp.einsum("yzn,nk->yzk", physical, sin_x, precision=HIGHEST)
        halfway = jnp.stack([real_half, imag_half])
        pieces = lax.all_to_all(halfway, "xz", split_axis=3, concat_axis=2, tiled=True)
        with_cos = jnp.einsum("cyzk,zq->cykq", pieces, cos_z, precision=HIGHEST)
        with_sin = jnp.einsum("cyzk,zq->cykq", pieces, sin_z, precision=HIGHEST)
        return jnp.stack([with_cos[0] + with_sin[1], with_cos[1] - with_sin[0]])

    def to_physical(spectral):
        with_cos = jnp.einsum("cykq,qz->cykz", spectral, cos_z, precision=HIGHEST)
        with_sin = jnp.einsum("cykq,qz->cykz", spectral, sin_z, precision=HIGHEST)
        halfway = jnp.stack([with_cos[0] - with_sin[1], with_sin[0] + with_cos[1]])
        pieces = lax.all_to_all(halfway, "xz", split_axis=3, concat_axis=2, tiled=True)
        return jnp.einsum("ykz,nk->yzn", pieces[0], cos_x, precision=HIGHEST) - jnp.einsum(
            "ykz,nk->yzn", pieces[1], sin_x, precision=HIGHEST
        )

    def begin(drag_rate, control):
        def drag_map(s):
            return to_spectral(drag_rate * to_physical(s))

        return drag_map, (lambda s: (drag_map(s), to_spectral(control[None])[:, 0]))

    def plane(spectral):
        return to_physical(spectral[:, None])[0]

    return begin, plane


def rotate(spectrum, factor):
    return jnp.stack([-factor * spectrum[1], factor * spectrum[0]])


def per_device(initial_state, drag_rate, wall_control, lift_profile, schur_inverse):
    row_count = initial_state.shape[2]
    mode_count = initial_state.shape[3]
    span_count = initial_state.shape[4]
    stream_len = drag_rate.shape[2]
    last_row = row_count - 1
    slab_count = lax.axis_size("gy")
    slab_index = lax.axis_index("gy")
    pencil_count = lax.axis_size("xz")
    pencil_index = lax.axis_index("xz")
    mode_ids = pencil_index * mode_count + jnp.arange(mode_count)
    stream_factor = (2.0 * math.pi / stream_len * mode_ids.astype(jnp.float32))[:, None]
    mode_weight = jnp.where(mode_ids == 0, 1.0, 2.0).astype(jnp.float32)[:, None]
    span_ids = jnp.arange(span_count)
    signed = jnp.where(span_ids < span_count // 2, span_ids, span_ids - span_count)
    span_wave = jnp.where(
        span_ids == span_count // 2, 0.0, 2.0 * math.pi / span_count * signed.astype(jnp.float32)
    )
    wave_square = stream_factor**2 + span_wave[None, :] ** 2
    fits = (
        slab_count == 2
        and QUAD * mode_count == LANES
        and QUAD * drag_rate.shape[1] == LANES
        and row_count == SUBLANES
        and pencil_count * mode_count * 2 == stream_len
        and pencil_count * drag_rate.shape[1] == span_count
        and pencil_count & (pencil_count - 1) == 0
        and pencil_count % QUAD == 0
    )
    if fits:
        return fused_call(pencil_count, initial_state, drag_rate, wall_control, lift_profile, schur_inverse)
    begin, plane = plain_transforms(pencil_count, row_count, mode_count, span_count, stream_len)
    drag_map, first_map = begin(drag_rate, wall_control)

    ends = slab_count - 1

    def from_above(tail):
        return lax.ppermute(tail, "gy", [(i, i + 1) for i in range(ends)])

    def from_below(head):
        return lax.ppermute(head, "gy", [(i + 1, i) for i in range(ends)])

    def every_slab(values):
        if slab_count == 2:
            other = lax.ppermute(values, "gy", [(0, 1), (1, 0)])
            return [jnp.where(slab_index == 0, values, other), jnp.where(slab_index == 0, other, values)]
        gathered = lax.all_gather(values, "gy", axis=0)
        return [gathered[i] for i in range(slab_count)]

    has_above = (slab_index > 0).astype(jnp.float32)
    has_below = (slab_index < slab_count - 1).astype(jnp.float32)
    corners = every_slab(
        jnp.stack(
            [
                schur_inverse[0, 0],
                schur_inverse[0, last_row],
                schur_inverse[last_row, 0],
                schur_inverse[last_row, last_row],
            ]
        )
    )
    corner_above = jnp.zeros_like(corners[0][3])
    for member in range(slab_count - 1):
        corner_above = jnp.where(slab_index == member + 1, corners[member][3], corner_above)

    padded_lift = jnp.pad(lift_profile, 1)
    lift_near = lax.dynamic_slice_in_dim(padded_lift, slab_index * row_count, row_count + 2)
    lift_own = lift_near[1 : row_count + 1]

    def halos(fields):
        tail = jnp.concatenate([fields[0, :, last_row:], fields[1, :, last_row - 1 :], fields[2, :, last_row:]], axis=1)
        head = jnp.concatenate([fields[0, :, :1], fields[1, :, :2], fields[2, :, :1]], axis=1)
        return from_above(tail), from_below(head)

    def smooth(wide):
        own = wide[:, 1:-1]
        laplace = wide[:, 2:] - 2.0 * own + wide[:, :-2]
        return own + DIFFUSION * (laplace - wave_square * own)

    def slope(wide):
        return 0.5 * (wide[:, 2:] - wide[:, :-2])

    def advance(fields, drag_term, control_hat):
        above, below = halos(fields)
        stream_star = smooth(jnp.concatenate([above[:, 0:1], fields[0], below[:, 0:1]], axis=1)) - drag_term
        span_star = smooth(jnp.concatenate([above[:, 3:4], fields[2], below[:, 3:4]], axis=1))
        normal_wide = smooth(jnp.concatenate([above[:, 1:3], fields[1], below[:, 1:3]], axis=1))
        if control_hat is not None:
            normal_wide = normal_wide + lift_near[:, None, None] * control_hat[:, None]
        normal_wide = jnp.concatenate(
            [has_above * normal_wide[:, :1], normal_wide[:, 1:-1], has_below * normal_wide[:, -1:]], axis=1
        )
        return stream_star, normal_wide[:, 1:-1], span_star, slope(normal_wide)

    def apply_blocks(values, transposed):
        summed = None
        for column in range(row_count):
            factor = schur_inverse[column] if transposed else schur_inverse[:, column]
            term = factor[None] * values[:, column : column + 1]
            summed = term if summed is None else summed + term
        return summed

    def solve(source, transposed):
        if transposed:
            first_column, last_column = schur_inverse[0], schur_inverse[last_row]
            ratio_at, turn_at = 1, 2
        else:
            first_column, last_column = schur_inverse[:, 0], schur_inverse[:, last_row]
            ratio_at, turn_at = 2, 1
        direct = apply_blocks(source, transposed)
        rims = every_slab(jnp.stack([direct[:, 0], direct[:, last_row]]))
        running = jnp.zeros_like(direct[:, 0])
        before = []
        for member in range(slab_count):
            before.append(running)
            running = rims[member][1] + corners[member][ratio_at][None] * running
        running = jnp.zeros_like(direct[:, 0])
        behind = [running] * slab_count
        for member in reversed(range(slab_count)):
            behind[member] = running
            top = rims[member][0] + corners[member][0][None] * before[member]
            running = top + corners[member][turn_at][None] * running
        entering, leaving = before[0], behind[0]
        for member in range(1, slab_count):
            entering = jnp.where(slab_index == member, before[member], entering)
            leaving = jnp.where(slab_index == member, behind[member], leaving)
        pressure = direct + first_column[None] * entering[:, None] + last_column[None] * leaving[:, None]
        row_above = entering + corner_above[None] * pressure[:, 0]
        return jnp.concatenate([row_above[:, None], pressure, leaving[:, None]], axis=1)

    def project(stream_part, normal_part, span_part, normal_slope, transposed):
        divergence = rotate(stream_part, stream_factor) + normal_slope + rotate(span_part, span_wave)
        wide = solve(divergence, transposed)
        pressure = wide[:, 1:-1]
        return jnp.stack(
            [
                stream_part - rotate(pressure, stream_factor),
                normal_part - slope(wide),
                span_part - rotate(pressure, span_wave),
            ]
        )

    fields = initial_state
    control_hat = None
    for section_index in range(STEPS):
        weighted = mode_weight * fields[0]
        if section_index == 0:
            drag_term, control_hat = first_map(weighted)
        else:
            drag_term = drag_map(weighted)
        fields = project(*advance(fields, drag_term, control_hat), False)
    final = fields
    normal_slope = slope(
        jnp.concatenate([from_above(final[1, :, last_row:]), final[1], from_below(final[1, :, :1])], axis=1)
    )
    parts = (final[0], final[1], final[2], normal_slope)
    wall_sum = jnp.zeros_like(control_hat)
    for section_index in range(STEPS):
        projected = project(*parts, True)
        wall_sum = wall_sum + jnp.sum(lift_own[:, None, None] * projected[1], axis=1)
        if section_index + 1 < STEPS:
            parts = advance(projected, mode_weight * drag_map(projected[0]), None)
    share = plane(wall_sum)
    if slab_count == 2:
        half = stream_len // 2
        first, second = share[:, :half], share[:, half:]
        upper = slab_index == 0
        other = lax.ppermute(jnp.where(upper, second, first), "gy", [(0, 1), (1, 0)])
        control_gradient = jnp.where(upper, first, second) + other
    else:
        control_gradient = lax.psum_scatter(share, "gy", scatter_dimension=1, tiled=True)
    return (final, control_gradient)


def solution(mesh):
    return jax.shard_map(
        per_device,
        mesh=mesh,
        in_specs=(
            P(None, None, "gy", "xz", None),
            P("gy", "xz", None),
            P("xz", None),
            P(),
            P("gy", None, "xz", None),
        ),
        out_specs=(P(None, None, "gy", "xz", None), P("xz", "gy")),
        check_vma=False,
    )
```

profile of v0, /device:TPU:0, one launch (start us, length us, event | category | flops | bytes accessed | tf_op | source)
XLA Modules:
  0.0 184.1 jit_solution(16512589015636144920)
XLA Ops:
  0.6 178.7 %shard_map.95 = (f32[3,2,8,2,16,512]{5,4,3,2,1,0:T(8,128)}, f32[32,512]{1,0:T(8,128)}) custom-call(f32[16]{0:T(128)} %refs_0_.1, f32[3,2,8,2,16,512]{5,4,3,2,1,0:T(8,128)} %bitcast.5, f32[8,32,1024]{2,1,0:T(8,128)} %refs_2_.1, f32[32,1024]{1,0:T(8,128)} %refs_3_.1, f32[8,8,2,16,512]{4,3,2,1,0:T(8,128)} %bitcast.4, ...), custom_call_target="tpu_custom_call" | custom-call | flops 60000002048 | bytes 32000000 | tf_op jit(solution)/shard_map/pallas_call | solution.py:637
  179.3 0.0 copy-start
  179.3 4.1 %copy.12 = f32[3,2,8,32,512]{4,3,2,1,0:T(8,128)} copy(f32[3,2,8,32,512]{4,3,2,1,0:T(8,128)} %bitcast.3) | data formatting | bytes 6291456
  183.5 0.0 copy-done
  183.5 0.6 copy.13
Async XLA Ops:
  179.3 4.1 %copy-start = (f32[32,512]{1,0:T(8,128)S(1)}, f32[32,512]{1,0:T(8,128)}, u32[]{:S(2)}) copy-start(f32[32,512]{1,0:T(8,128)} %get-tuple-element.9) | copy-start | bytes 196612
where the time goes:
time: 184 us
  Pallas kernels  179 us (97%)
  local copies, waits for them, and re-layouts  4.76 us (3%)
    pallas_call x1, Pallas kernels, fused_call(): pl.pallas_call(functools.partial(fused_kernel, count, stream_len), out_sh...  179 us
    unnamed x4, local copies, waits for them, and re-layouts  4.76 us

commit v1 on v0

--- a/solution.py
+++ b/solution.py
@@ -20,6 +20,8 @@
 QUAD = 4
 HALVES = 2
 SUBLANES = 8
+FAR_FIRST = (3, 2, 0, 1)
+VMEM_BYTES = 67_043_328
 
 
 def split_host(table):
@@ -111,47 +113,45 @@
 
 
 class Exchange:
-    def __init__(self, count, me, outbox, inbox, send_sem, recv_sem):
-        self.count, self.me = count, me
+    def __init__(self, peers, me, outbox, inbox, send_sem, recv_sem):
+        self.peers, self.me = peers, me
         self.outbox, self.inbox, self.send_sem, self.recv_sem = outbox, inbox, send_sem, recv_sem
 
-    def copy(self, peer, slot):
+    def copy(self, src, dst, peer):
         return pltpu.make_async_remote_copy(
-            src_ref=self.outbox.at[peer],
-            dst_ref=self.inbox.at[slot],
-            send_sem=self.send_sem.at[peer],
-            recv_sem=self.recv_sem.at[slot],
+            src_ref=self.outbox.at[src],
+            dst_ref=self.inbox.at[dst],
+            send_sem=self.send_sem,
+            recv_sem=self.recv_sem,
             device_id={"xz": peer},
             device_id_type=MESH,
         )
 
-    def loop(self, action):
-        def body(step, carry):
-            action(peer_at(self.count, self.me, step))
-            return carry
-
-        lax.fori_loop(1, self.count, body, 0)
+    def every(self):
+        others = pl.ds(0, len(self.peers))
+        return self.copy(others, others, self.peers[0])
 
     def start(self):
-        self.loop(lambda peer: self.copy(peer, self.me).start())
+        for peer in self.peers:
+            self.copy(peer, self.me, peer).start()
         self.inbox[self.me] = self.outbox[self.me]
 
     def arrive(self):
-        self.loop(lambda peer: self.copy(peer, peer).wait_recv())
+        self.every().wait_recv()
 
     def finish(self):
-        self.loop(lambda peer: self.copy(peer, peer).wait_send())
+        self.every().wait_send()
 
 
 def fused_kernel(count, stream_len, *refs):
     refs = list(refs)
     lift, state_far, drag_far, control_far, schur_far, span_far, inverse_far, forward_far = refs[:8]
-    final_far, gradient = refs[8:10]
+    final, gradient = refs[8:10]
     (
-        fields, final, base, source, drag_term, direct, schur, drag_raw, drag, control, control_hat,
+        fields, base, source, drag_term, direct, schur, drag_raw, drag, control, control_hat,
         span, inverse, forward, out1, in1, out2, in2, pair, damped, outc, inc, outp, inp,
-        halo_u, halo_v, halo_w, halo_final, rim, corner, wall, share, share_in,
-        load_sem, send_sem, recv_sem, plane_send, plane_recv, near_send, near_recv, store_sem,
+        halo_u, halo_v, halo_w, beyond, rim, corner, wall, reply, reply_rim, inp_other, share,
+        load_sem, send_sem, recv_sem, plane_send, plane_recv, near_send, near_recv,
     ) = refs[10:]
     me = lax.axis_index("xz")
     slab = lax.axis_index("gy")
@@ -163,8 +163,13 @@
     tiles = width // SUBLANES * tiles_q
     block = rows * width
     edge = (rows - 1) * (1 - slab)
+    edge_pair = (rows - 2) * (1 - slab)
+    edge_at = 1 - slab
     has_above = slab.astype(jnp.float32)
     has_below = 1.0 - has_above
+    reach_up = [has_above * lift[slab * (rows - 1)]] + [lift[slab * rows + y] for y in range(rows - 1)]
+    reach_down = [lift[slab * rows + y] for y in range(1, rows)] + [has_below * lift[rows]]
+    lift_slope = [0.5 * (down - up) for up, down in zip(reach_up, reach_down)]
 
     loads = {
         "stream": (state_far.at[0], fields.at[0]),
@@ -179,24 +184,26 @@
     loads = {
         name: pltpu.make_async_copy(far, near, load_sem.at[i]) for i, (name, (far, near)) in enumerate(loads.items())
     }
-    for load in loads.values():
-        load.start()
-
+    loads["stream"].start()
+    loads["span"].start()
+    order = sorted(range(1, count), key=lambda step: (FAR_FIRST[step * QUAD // count], -step))
+    peers = [peer_at(count, me, step) for step in order]
     barrier = pltpu.get_barrier_semaphore()
-
-    def greet(step, carry):
-        pl.semaphore_signal(barrier, inc=1, device_id={"xz": peer_at(count, me, step)}, device_id_type=MESH)
-        return carry
-
-    lax.fori_loop(1, count, greet, 0)
+    for peer in peers:
+        pl.semaphore_signal(barrier, inc=1, device_id={"xz": peer}, device_id_type=MESH)
     pl.semaphore_signal(barrier, inc=1, device_id={"gy": 1 - slab}, device_id_type=MESH)
-    pl.semaphore_wait(barrier, count)
 
     def first(h, g):
-        return Exchange(count, me, out1.at[h, g], in1.at[h, g], send_sem.at[0, h, g], recv_sem.at[0, h, g])
+        return Exchange(peers, me, out1.at[h, g], in1.at[h, g], send_sem.at[0, h, g], recv_sem.at[0, h, g])
 
     def second(h, g):
-        return Exchange(count, me, out2.at[h, g], in2.at[h, g], send_sem.at[1, h, g], recv_sem.at[1, h, g])
+        return Exchange(peers, me, out2.at[h, g], in2.at[h, g], send_sem.at[1, h, g], recv_sem.at[1, h, g])
+
+    def third(h):
+        return Exchange(peers, me, outc.at[h], inc.at[h], plane_send.at[0, h], plane_recv.at[0, h])
+
+    def fourth(h):
+        return Exchange(peers, me, outp.at[h], inp.at[h], plane_send.at[1, h], plane_recv.at[1, h])
 
     def across(src, dst, index):
         return pltpu.make_async_remote_copy(
@@ -209,24 +216,20 @@
         )
 
     def halo_copies(h):
-        pair_row = (rows - 2) * (1 - slab)
         return [
             across(fields.at[0, :, edge, h], halo_u.at[h], h),
-            across(fields.at[1, :, pl.ds(pair_row, 2), h], halo_v.at[h], HALVES + h),
+            across(fields.at[1, :, pl.ds(edge_pair, 2), h], halo_v.at[h], HALVES + h),
             across(fields.at[2, :, edge, h], halo_w.at[h], 2 * HALVES + h),
         ]
 
-    def rim_copy(h):
-        return across(direct.at[:, edge], rim.at[h], 3 * HALVES + h)
-
-    def final_copy(h):
-        return across(final.at[1, :, edge, h], halo_final.at[h], 4 * HALVES + h)
-
-    corner_copy = across(schur.at[edge, edge], corner, 5 * HALVES)
-    share_copy = across(share.at[1 - slab], share_in, 5 * HALVES + 1)
-
-    def store_copy(h):
-        return pltpu.make_async_copy(final.at[:, :, :, h], final_far.at[:, :, :, h], store_sem.at[h])
+    def rim_copy(h, turn):
+        return across(direct.at[:, pl.ds(edge_pair, 2)], rim.at[turn, h], (3 + turn) * HALVES + h)
+
+    def plane_copy(h):
+        return across(inp.at[h], inp_other.at[h], 5 * HALVES + h)
+
+    corner_copy = across(schur.at[pl.ds(edge_pair, 2), edge], corner, 6 * HALVES)
+    reply_copy = across(reply.at[edge], reply_rim, 6 * HALVES + 1)
 
     def every_half(action):
         def body(h, carry):
@@ -261,7 +264,7 @@
     def mode_weight(h, sub):
         return jnp.where(mode_ids(h, sub) == 0, 1.0, 2.0)
 
-    def send_first(h, weighted):
+    def pack_first(h, weighted):
         x = fields[0, :, :, h]
         if weighted:
             ids = me * modes + h * width + lax.broadcasted_iota(jnp.int32, x.shape, 2)
@@ -279,15 +282,26 @@
                     parts = [halfway[part][start + width * y : start + width * (y + 1), lanes] for y in range(QUAD)]
                     for i, tile in enumerate(swap_groups(parts)):
                         out1[h, g, QUAD * group + i, part] = tile
-            first(h, g).start()
+
+    def send_first(h, weighted):
+        pack_first(h, weighted)
+        first(h, 0).start()
+
+        @pl.when(h == 0)
+        def _():
+            for g in range(1, chunks):
+                first(0, g).start()
 
     def physical(again):
+        first(1, 0).finish()
+        for g in range(1, chunks):
+            first(1, g).start()
         for g in range(chunks):
             for h in range(HALVES):
                 first(h, g).arrive()
                 fill_pair(pair, slice(h * block * 4, (h + 1) * block * 4), in1[h, g].reshape(-1, LANES))
-                if again:
-                    second(h, g).finish()
+            if again:
+                second(1, g).finish()
 
             def damp(index, at, y):
                 fill_pair(damped, at, y * drag[g, at, :])
@@ -299,14 +313,26 @@
 
             stream_product(forward, damped, keep)
             second(0, g).start()
-        for h in range(1, HALVES):
-            for g in range(chunks):
-                second(h, g).start()
+        for g in range(chunks):
+            first(0, g).finish()
+            if g:
+                first(1, g).finish()
+
+    def send_rest():
+        second(0, 0).finish()
+        second(1, 0).start()
+        for g in range(1, chunks):
+            second(0, g).finish()
 
     def collect(h):
         for g in range(chunks):
             second(h, g).arrive()
-            first(h, g).finish()
+
+        @pl.when(h == 0)
+        def _():
+            for g in range(1, chunks):
+                second(1, g).start()
+
         parts = []
         for part in range(2):
             for g in range(chunks):
@@ -347,6 +373,12 @@
                     places = [slab * (rows - 1)] + [slab * rows + y for y in range(rows)] + [rows]
                     lines = [line + lift[place] * hat for line, place in zip(lines, places)]
                 lines = [has_above * lines[0]] + lines[1:-1] + [has_below * lines[-1]]
+                beyond[(h, p) + at] = lines[0] + lines[-1]
+                if not forced:
+                    total = wall[(p, h) + at]
+                    for y in range(rows):
+                        total = total + lift[slab * rows + y] * lines[y + 1]
+                    wall[(p, h) + at] = total
                 sign = -1.0 if p == 0 else 1.0
                 for y in range(rows):
                     base[(0, p, y, h) + at] = stream[p][y]
@@ -369,56 +401,35 @@
             for p in range(2):
                 direct[(p, i) + at] = totals[p]
 
-    def begin_solve(h, transposed):
+    def begin_solve(h):
         def body(at, sub, column):
             kx, _ = waves(h, sub, column)
-            if transposed:
-                kx = kx * mode_weight(h, sub)
             values = [
                 [source[(0, y, h) + at] + kx * drag_term[(1, y) + at] for y in range(rows)],
                 [source[(1, y, h) + at] - kx * drag_term[(0, y) + at] for y in range(rows)],
             ]
-            apply_blocks(h, at, values, transposed)
+            apply_blocks(h, at, values, False)
 
         every_tile(body)
 
-    def begin_adjoint(h):
-        def body(at, sub, column):
-            kx, kz = waves(h, sub, column)
-            values = []
-            for p in range(2):
-                line = halo_final[(h, p) + at]
-                lines = [has_above * line] + [final[(1, p, y, h) + at] for y in range(rows)] + [has_below * line]
-                sign = -1.0 if p == 0 else 1.0
-                values.append(
-                    [
-                        sign * (kx * final[(0, 1 - p, y, h) + at] + kz * final[(2, 1 - p, y, h) + at])
-                        + 0.5 * (lines[y + 2] - lines[y])
-                        for y in range(rows)
-                    ]
-                )
-            apply_blocks(h, at, values, True)
-
-        every_tile(body)
-
-    def swap_rims(h):
-        copy = rim_copy(h)
+    def swap_rims(h, turn):
+        copy = rim_copy(h, turn)
         copy.start()
         copy.wait_recv()
         copy.wait_send()
 
     def pressure_at(h, at, transposed):
-        turn = corner[(h,) + at]
+        turn = corner[(1 - edge_at, h) + at]
         reach = [schur[((edge, i) if transposed else (i, edge)) + (h,) + at] for i in range(rows)]
         own = schur[(edge, edge, h) + at]
         wide = []
         for p in range(2):
-            near = direct[(p, edge) + at]
-            far = rim[(h, p) + at]
-            outer = far + has_below * (turn * near)
-            above = has_above * (far + turn * (near + own * far))
+            far = rim[(int(transposed), h, p, 1 - edge_at) + at]
+            known = direct[(p, edge) + at] + has_above * (own * far)
+            next_row = far + turn * known
+            outer = has_above * far + has_below * next_row
             inside = [direct[(p, y) + at] + reach[y] * outer for y in range(rows)]
-            wide.append([above] + inside + [has_below * outer])
+            wide.append([has_above * next_row] + inside + [has_below * next_row])
         return wide
 
     def finish_solve(h, target):
@@ -436,7 +447,54 @@
 
         every_tile(body)
 
-    def finish_adjoint(h, last):
+    def finish_and_reverse(h):
+        def body(at, sub, column):
+            kx, kz = waves(h, sub, column)
+            wide = pressure_at(h, at, False)
+            turn = corner[(edge_at, h) + at]
+            own = schur[(edge, edge, h) + at]
+            stream, normal, across_span = [], [], []
+            for p in range(2):
+                sign = 1.0 if p == 0 else -1.0
+                far = rim[(0, h, p, 1 - edge_at) + at]
+                known = direct[(p, edge) + at] + has_above * (own * far)
+                inner_row = rim[(0, h, p, edge_at) + at] + turn * known
+                edge_row = has_below * wide[p][rows] + has_above * wide[p][1]
+                outside = beyond[(h, p) + at] + 0.5 * (has_above - has_below) * (inner_row - edge_row)
+                lines = [has_above * outside]
+                for y in range(rows):
+                    turned = sign * wide[1 - p][y + 1]
+                    slope = 0.5 * (wide[p][y + 2] - wide[p][y])
+                    stream.append(base[(0, p, y, h) + at] - drag_term[(p, y) + at] + kx * turned)
+                    lines.append(base[(1, p, y, h) + at] - slope)
+                    across_span.append(base[(2, p, y, h) + at] + kz * turned)
+                    final[(0, p, y, h) + at] = stream[-1]
+                    final[(1, p, y, h) + at] = lines[-1]
+                    final[(2, p, y, h) + at] = across_span[-1]
+                normal.append(lines + [has_below * outside])
+            values = []
+            for p in range(2):
+                sign = -1.0 if p == 0 else 1.0
+                values.append(
+                    [
+                        sign * (kx * stream[rows * (1 - p) + y] + kz * across_span[rows * (1 - p) + y])
+                        + 0.5 * (normal[p][y + 2] - normal[p][y])
+                        for y in range(rows)
+                    ]
+                )
+            for p in range(2):
+                for y in range(rows):
+                    source[(p, y, h) + at] = values[p][y]
+
+        every_tile(body)
+
+        def reverse(at, sub, column):
+            values = [[source[(p, y, h) + at] for y in range(rows)] for p in range(2)]
+            apply_blocks(h, at, values, True)
+
+        every_tile(reverse)
+
+    def finish_adjoint(h):
         def body(at, sub, column):
             kx, kz = waves(h, sub, column)
             wide = pressure_at(h, at, True)
@@ -444,18 +502,58 @@
                 sign = 1.0 if p == 0 else -1.0
                 total = None
                 for y in range(rows):
-                    slope = 0.5 * (wide[p][y + 2] - wide[p][y])
-                    if last:
-                        normal = base[(1, p, y, h) + at] - slope
-                    else:
-                        turned = sign * wide[1 - p][y + 1]
-                        normal = final[(1, p, y, h) + at] - slope
-                        fields[(0, p, y, h) + at] = final[(0, p, y, h) + at] + kx * turned
-                        fields[(1, p, y, h) + at] = normal
-                        fields[(2, p, y, h) + at] = final[(2, p, y, h) + at] + kz * turned
+                    turned = sign * wide[1 - p][y + 1]
+                    normal = final[(1, p, y, h) + at] - 0.5 * (wide[p][y + 2] - wide[p][y])
+                    fields[(0, p, y, h) + at] = final[(0, p, y, h) + at] + kx * turned
+                    fields[(1, p, y, h) + at] = normal
+                    fields[(2, p, y, h) + at] = final[(2, p, y, h) + at] + kz * turned
                     term = lift[slab * rows + y] * normal
                     total = term if total is None else total + term
-                wall[(p, h) + at] = wall[(p, h) + at] + total if last else total
+                wall[(p, h) + at] = total
+
+        every_tile(body)
+
+    def start_reply():
+        def body(h):
+            def tile(at, sub, column):
+                for i in range(rows):
+                    total = None
+                    for j in range(rows):
+                        term = schur[(i, j, h) + at] * lift_slope[j]
+                        total = term if total is None else total + term
+                    reply[(i, h) + at] = total
+
+            every_tile(tile)
+
+        every_half(body)
+        reply_copy.start()
+
+    def finish_reply():
+        reply_copy.wait_recv()
+        reply_copy.wait_send()
+
+        def body(h):
+            def tile(at, sub, column):
+                far = reply_rim[(h,) + at]
+                outer = far + has_below * (corner[(1 - edge_at, h) + at] * reply[(edge, h) + at])
+                for y in range(rows):
+                    reply[(y, h) + at] = reply[(y, h) + at] + schur[(y, edge, h) + at] * outer
+
+            every_tile(tile)
+
+        every_half(body)
+
+    def close_wall(h):
+        def body(at, sub, column):
+            kx, _ = waves(h, sub, column)
+            kx = kx * mode_weight(h, sub)
+            for p in range(2):
+                sign = 1.0 if p == 0 else -1.0
+                total = wall[(p, h) + at]
+                for y in range(rows):
+                    value = source[(p, y, h) + at] + sign * (kx * drag_term[(1 - p, y) + at])
+                    total = total + reply[(y, h) + at] * value
+                wall[(p, h) + at] = total
 
         every_tile(body)
 
@@ -474,58 +572,63 @@
 
     loads["stream"].wait()
     loads["span"].wait()
-    every_half(lambda h: send_first(h, True))
+    for name in ("control", "forward", "rest", "schur", "drag", "inverse"):
+        loads[name].start()
+    pack_first(0, True)
+    pl.semaphore_wait(barrier, count)
+    for g in range(chunks):
+        first(0, g).start()
+    pack_first(1, True)
+    first(1, 0).start()
 
     loads["control"].wait()
     loads["forward"].wait()
-    third = Exchange(count, me, outc, inc, plane_send.at[0], plane_recv.at[0])
     lines = control[...]
     blank = jnp.zeros((LANES - lines.shape[0], stream_len), jnp.float32)
     fill_pair(pair, slice(None), jnp.concatenate([lines, blank], axis=0).T)
 
     def pack(index, at, y):
-        y = y.reshape(count, 2, HALVES, SUBLANES, LANES)
-        damped_rows = y[:, :, 0] + pltpu.roll(y[:, :, 1], LANES // QUAD, 3)
-
-        @pl.when(index == 0)
-        def _():
-            outc[...] = damped_rows
-
-        @pl.when(index != 0)
-        def _():
-            outc[...] = outc[...] + pltpu.roll(damped_rows, LANES // 2, 3)
+        y = y.reshape(count, QUAD, SUBLANES, LANES)
+        moved = y[:, 0]
+        for j in range(1, QUAD):
+            moved = moved + pltpu.roll(y[:, j], j * LANES // QUAD, 2)
+        outc[index] = moved
 
     stream_product(forward, pair, pack)
-    third.start()
+    every_half(lambda h: third(h).start())
     loads["rest"].wait()
     every_half(start_halos)
     loads["schur"].wait()
     corner_copy.start()
+    start_reply()
     loads["drag"].wait()
     for g in range(chunks):
         drag[g] = drag_raw[QUAD * g : QUAD * (g + 1)].reshape(LANES, stream_len).T
     loads["inverse"].wait()
     physical(False)
-    third.arrive()
-    parts = []
-    for part in range(2):
+
+    def control_half(h):
+        third(h).arrive()
         columns = []
         for group in range(groups):
-            pieces = [inc[QUAD * group + i, part] for i in range(QUAD)]
+            pieces = [inc[h, QUAD * group + i] for i in range(QUAD)]
             columns.append(jnp.concatenate(swap_groups(pieces), axis=0))
-        parts.append(jnp.concatenate(columns, axis=1))
-    w = span_product(jnp.concatenate(parts, axis=0), span)
-    shape = (HALVES, width, span_count)
-    control_hat[0] = (w[:modes, :span_count] + w[modes:, span_count:]).reshape(shape)
-    control_hat[1] = (w[modes:, :span_count] - w[:modes, span_count:]).reshape(shape)
+        w = span_product(jnp.concatenate(columns, axis=1), span)
+        control_hat[0, h] = w[:width, :span_count] + w[width:, span_count:]
+        control_hat[1, h] = w[width:, :span_count] - w[:width, span_count:]
+        third(h).finish()
+
+    every_half(control_half)
     corner_copy.wait_recv()
     corner_copy.wait_send()
+    finish_reply()
     spread_all(True)
+    send_rest()
 
     def step(h):
         collect(h)
-        begin_solve(h, False)
-        swap_rims(h)
+        begin_solve(h)
+        swap_rims(h, 0)
         finish_solve(h, fields)
         send_first(h, True)
         start_halos(h)
@@ -533,73 +636,65 @@
     every_half(step)
     physical(True)
     spread_all(True)
+    send_rest()
 
     def turn(h):
         collect(h)
-        begin_solve(h, False)
-        swap_rims(h)
-        finish_solve(h, final)
-        copy = final_copy(h)
-        copy.start()
-        store_copy(h).start()
-        copy.wait_recv()
-        copy.wait_send()
-        begin_adjoint(h)
-        swap_rims(h)
-        finish_adjoint(h, False)
+        begin_solve(h)
+        swap_rims(h, 0)
+        finish_and_reverse(h)
+        swap_rims(h, 1)
+        finish_adjoint(h)
         send_first(h, False)
         start_halos(h)
 
     every_half(turn)
     physical(True)
     spread_all(False)
+    send_rest()
 
     def close(h):
         collect(h)
-        begin_solve(h, True)
-        swap_rims(h)
-        finish_adjoint(h, True)
-
-    every_half(close)
-    fourth = Exchange(count, me, outp, inp, plane_send.at[1], plane_recv.at[1])
-    w = span_product(wall[...].reshape(2 * modes, span_count), span)
-    halfway = (
-        w[:modes, :span_count] - w[modes:, span_count:],
-        w[:modes, span_count:] + w[modes:, :span_count],
-    )
-    for part in range(2):
+        close_wall(h)
+        w = span_product(wall[:, h].reshape(2 * width, span_count), span)
+        halfway = (
+            w[:width, :span_count] - w[width:, span_count:],
+            w[:width, span_count:] + w[width:, :span_count],
+        )
         for group in range(groups):
             lanes = slice(LANES * group, LANES * (group + 1))
-            pieces = [halfway[part][SUBLANES * j : SUBLANES * (j + 1), lanes] for j in range(QUAD)]
+            pieces = [half[at : at + SUBLANES, lanes] for half in halfway for at in range(0, width, SUBLANES)]
             for i, tile in enumerate(swap_groups(pieces)):
-                outp[QUAD * group + i, part] = tile
-    fourth.start()
-    fourth.arrive()
-    x = inp[...]
-    turned = [x] + [pltpu.roll(x, LANES - j * LANES // QUAD, 3) for j in range(1, QUAD)]
+                outp[h, QUAD * group + i] = tile
+        fourth(h).start()
+
+    def open_plane(h):
+        fourth(h).arrive()
+        copy = plane_copy(h)
+        copy.start()
+        copy.wait_recv()
+        copy.wait_send()
+        x = inp[h] + inp_other[h]
+        turned = [x] + [pltpu.roll(x, LANES - j * LANES // QUAD, 2) for j in range(1, QUAD)]
+        x = jnp.concatenate(turned, axis=1).reshape(-1, LANES)
+        terms = slice(h * x.shape[0], (h + 1) * x.shape[0])
+        fill_pair(pair, terms, x)
+        places = pl.ds(pl.multiple_of(slab * gradient.shape[1], LANES), gradient.shape[1])
+        y = mxu(inverse[0, places, terms], pair[terms, :])
+        return y[:, :LANES] + (y[:, LANES:] + mxu(inverse[1, places, terms], pair[terms, :LANES]))
+
+    every_half(close)
+    share[...] = open_plane(0)
+    gradient[...] = (share[...] + open_plane(1)).T[: gradient.shape[0]]
     for h in range(HALVES):
-        both = jnp.concatenate(turned[2 * h : 2 * h + 2], axis=2)
-        fill_pair(pair, slice(h * block * 4, (h + 1) * block * 4), both.reshape(-1, LANES))
-
-    def keep_share(index, at, y):
-        share[index] = y.T[: share.shape[1]]
-
-    stream_product(inverse, pair, keep_share)
-    share_copy.start()
-    third.finish()
-    fourth.finish()
-    for h in range(HALVES):
-        store_copy(h).wait()
-        for g in range(chunks):
-            second(h, g).finish()
-    share_copy.wait_recv()
-    share_copy.wait_send()
-    gradient[...] = share[slab] + share_in[...]
+        fourth(h).finish()
+    for g in range(chunks):
+        second(1, g).finish()
 
 
 VMEM = pl.BlockSpec(memory_space=pltpu.VMEM)
 SMEM = pl.BlockSpec(memory_space=pltpu.SMEM)
-FAR = pl.BlockSpec(memory_space=pl.ANY)
+FAR = pl.BlockSpec(memory_space=pltpu.HBM)
 
 
 def fused_call(count, initial_state, drag_rate, wall_control, lift_profile, schur_inverse):
@@ -614,37 +709,39 @@
     plane = (2, rows, HALVES, width, span_count)
     half_plane = (2, rows, width, span_count)
     box = (HALVES, chunks, count, 2, width, LANES)
-    thin = (count, 2, SUBLANES, LANES)
+    thin = (HALVES, count, SUBLANES, LANES)
     line = (HALVES, 2, width, span_count)
+
+    kept = 4 * (math.prod(state.shape) + narrow * stream_len // 2 + 16 * SUBLANES * LANES)
 
     def buffer(*shape):
         return pltpu.VMEM(shape, jnp.float32)
 
     pairs = pltpu.VMEM((stream_len, 2 * LANES), jnp.bfloat16)
-    scratch = [buffer(*state.shape)] * 3 + [buffer(*plane), buffer(*half_plane), buffer(*half_plane)]
+    scratch = [buffer(*state.shape)] * 2 + [buffer(*plane), buffer(*half_plane), buffer(*half_plane)]
     scratch += [buffer(*schur.shape), buffer(*drag_rate.shape), buffer(chunks, stream_len, LANES)]
     scratch += [buffer(*wall_control.shape), buffer(*line)]
     scratch += [pltpu.VMEM(table.shape, jnp.bfloat16) for table in (span, inverse, forward)]
     scratch += [buffer(*box)] * 4 + [pairs] * 2 + [buffer(*thin)] * 4
-    scratch += [buffer(*line), buffer(HALVES, 2, 2, width, span_count), buffer(*line), buffer(*line), buffer(*line)]
-    scratch += [buffer(HALVES, width, span_count), buffer(*line)]
-    scratch += [buffer(2, narrow, stream_len // 2), buffer(narrow, stream_len // 2)]
+    scratch += [buffer(*line), buffer(HALVES, 2, 2, width, span_count), buffer(*line), buffer(*line)]
+    scratch += [buffer(2, HALVES, 2, 2, width, span_count), buffer(2, HALVES, width, span_count), buffer(*line)]
+    scratch += [buffer(rows, HALVES, width, span_count), buffer(HALVES, width, span_count)]
+    scratch += [buffer(*thin), buffer(stream_len // 2, LANES)]
     scratch += [pltpu.SemaphoreType.DMA((8,))]
-    scratch += [pltpu.SemaphoreType.DMA((2, HALVES, chunks, count))] * 2
-    scratch += [pltpu.SemaphoreType.DMA((2, count))] * 2
-    scratch += [pltpu.SemaphoreType.DMA((5 * HALVES + 2,))] * 2
-    scratch += [pltpu.SemaphoreType.DMA((HALVES,))]
+    scratch += [pltpu.SemaphoreType.DMA((2, HALVES, chunks))] * 2
+    scratch += [pltpu.SemaphoreType.DMA((2, HALVES))] * 2
+    scratch += [pltpu.SemaphoreType.DMA((6 * HALVES + 2,))] * 2
     final, gradient = pl.pallas_call(
         functools.partial(fused_kernel, count, stream_len),
         out_shape=[
-            jax.ShapeDtypeStruct(state.shape, jnp.float32),
-            jax.ShapeDtypeStruct((narrow, stream_len // 2), jnp.float32),
+            pltpu.VMEM(state.shape, jnp.float32),
+            pltpu.VMEM((narrow, stream_len // 2), jnp.float32),
         ],
         in_specs=[SMEM] + [FAR] * 7,
-        out_specs=[FAR, VMEM],
+        out_specs=[VMEM, VMEM],
         scratch_shapes=scratch,
         compiler_params=pltpu.CompilerParams(
-            collective_id=0, has_side_effects=True, vmem_limit_bytes=63 * 1024 * 1024
+            collective_id=0, has_side_effects=True, vmem_limit_bytes=VMEM_BYTES - kept
         ),
         cost_estimate=pl.CostEstimate(flops=60_000_000_000, bytes_accessed=32_000_000, transcendentals=0),
     )(lift_profile, state, drag_rate, wall_control, schur, span, inverse, forward)

time: 184 us -> 162 us (0.88)
  Pallas kernels: 179 us -> 159 us
  local copies, waits for them, and re-layouts: 4.76 us -> 2.3 us
    pallas_call x1, Pallas kernels: 179 us -> 159 us  [fused_call(): pl.pallas_call(functools.partial(fused_kernel, count, stream_len), out_sh...]
    unnamed x4 -> x2, local copies, waits for them, and re-layouts: 4.76 us -> 2.3 us
where the time goes in v1:
time: 162 us
  Pallas kernels  159 us (98%)
  local copies, waits for them, and re-layouts  2.3 us (1%)
    pallas_call x1, Pallas kernels, fused_call(): pl.pallas_call(functools.partial(fused_kernel, count, stream_len), out_sh...  159 us

profile of v1, /device:TPU:0, one launch (start us, length us, event | category | flops | bytes accessed | tf_op | source)
XLA Modules:
  0.0 161.9 jit_solution(5307139041606645208)
XLA Ops:
  0.6 159.0 %shard_map.95 = (f32[3,2,8,2,16,512]{5,4,3,2,1,0:T(8,128)S(1)}, f32[32,512]{1,0:T(8,128)S(1)}) custom-call(f32[16]{0:T(128)} %refs_0_.1, f32[3,2,8,2,16,512]{5,4,3,2,1,0:T(8,128)} %bitcast.5, f32[8,32,1024]{2,1,0:T(8,128)} %refs_2_.1, f32[32,1024]{1,0:T(8,128)} %refs_3_.1, f32[8,8,2,16,512]{4,3,2,1,0:T(8,128)} %bitcast.4, ...), custom_call_target="tpu_custom_call" | custom-call | flops 60000002048 | bytes 32000000 | tf_op jit(solution)/shard_map/pallas_call | solution.py:734
  159.7 1.7 %copy.12 = f32[3,2,8,32,512]{4,3,2,1,0:T(8,128)} copy(f32[3,2,8,32,512]{4,3,2,1,0:T(8,128)S(1)} %bitcast.3) | data formatting | bytes 6291456
  161.3 0.6 copy.13

commit v2 on v1

--- a/solution.py
+++ b/solution.py
@@ -58,17 +58,10 @@
     return both[: x.shape[0]] + (both[x.shape[0] :] + mxu(high, table[1]))
 
 
-def stream_product(table, pair, store):
-    tile = table.shape[1] // HALVES
-
-    def body(index, carry):
-        rows = pl.ds(pl.multiple_of(index * tile, tile), tile)
-        wide = mxu(table[0, rows, :], pair[...])
-        narrow = mxu(table[1, rows, :], pair[:, :LANES])
-        store(index, rows, wide[:, :LANES] + (wide[:, LANES:] + narrow))
-        return carry
-
-    lax.fori_loop(0, HALVES, body, 0)
+def split_product(table, rows, terms, pair):
+    wide = mxu(table[0, rows, terms], pair[...])
+    narrow = mxu(table[1, rows, terms], pair[:, :LANES])
+    return wide[:, :LANES] + (wide[:, LANES:] + narrow)
 
 
 def fill_pair(pair, rows, x):
@@ -145,11 +138,11 @@
 
 def fused_kernel(count, stream_len, *refs):
     refs = list(refs)
-    lift, state_far, drag_far, control_far, schur_far, span_far, inverse_far, forward_far = refs[:8]
+    lift_far, state_far, drag_far, control_far, schur_far, span_far, inverse_far, forward_far = refs[:8]
     final, gradient = refs[8:10]
     (
-        fields, base, source, drag_term, direct, schur, drag_raw, drag, control, control_hat,
-        span, inverse, forward, out1, in1, out2, in2, pair, damped, outc, inc, outp, inp,
+        lift, fields, base, source, drag_term, direct, schur, drag_raw, drag, control, control_hat,
+        span, inverse, forward, out1, in1, out2, in2, pair, damped, partial, outc, inc, outp, inp,
         halo_u, halo_v, halo_w, beyond, rim, corner, wall, reply, reply_rim, inp_other, share,
         load_sem, send_sem, recv_sem, plane_send, plane_recv, near_send, near_recv,
     ) = refs[10:]
@@ -167,9 +160,6 @@
     edge_at = 1 - slab
     has_above = slab.astype(jnp.float32)
     has_below = 1.0 - has_above
-    reach_up = [has_above * lift[slab * (rows - 1)]] + [lift[slab * rows + y] for y in range(rows - 1)]
-    reach_down = [lift[slab * rows + y] for y in range(1, rows)] + [has_below * lift[rows]]
-    lift_slope = [0.5 * (down - up) for up, down in zip(reach_up, reach_down)]
 
     loads = {
         "stream": (state_far.at[0], fields.at[0]),
@@ -180,6 +170,7 @@
         "drag": (drag_far, drag_raw),
         "rest": (state_far.at[1:3], fields.at[1:3]),
         "schur": (schur_far, schur),
+        "lift": (lift_far, lift),
     }
     loads = {
         name: pltpu.make_async_copy(far, near, load_sem.at[i]) for i, (name, (far, near)) in enumerate(loads.items())
@@ -199,8 +190,7 @@
     def second(h, g):
         return Exchange(peers, me, out2.at[h, g], in2.at[h, g], send_sem.at[1, h, g], recv_sem.at[1, h, g])
 
-    def third(h):
-        return Exchange(peers, me, outc.at[h], inc.at[h], plane_send.at[0, h], plane_recv.at[0, h])
+    third = Exchange(peers, me, outc, inc, plane_send.at[0, 0], plane_recv.at[0, 0])
 
     def fourth(h):
         return Exchange(peers, me, outp.at[h], inp.at[h], plane_send.at[1, h], plane_recv.at[1, h])
@@ -229,6 +219,7 @@
         return across(inp.at[h], inp_other.at[h], 5 * HALVES + h)
 
     corner_copy = across(schur.at[pl.ds(edge_pair, 2), edge], corner, 6 * HALVES)
+    control_copy = across(control_hat.at[:, slab], control_hat.at[:, slab], 6 * HALVES + 2)
     reply_copy = across(reply.at[edge], reply_rim, 6 * HALVES + 1)
 
     def every_half(action):
@@ -264,21 +255,22 @@
     def mode_weight(h, sub):
         return jnp.where(mode_ids(h, sub) == 0, 1.0, 2.0)
 
-    def pack_first(h, weighted):
-        x = fields[0, :, :, h]
+    def pack_first(h, weighted, low=0, high=chunks):
+        x = fields[0, :, QUAD * low : QUAD * high, h]
         if weighted:
             ids = me * modes + h * width + lax.broadcasted_iota(jnp.int32, x.shape, 2)
             x = x * jnp.where(ids == 0, 1.0, 2.0)
-        w = span_product(x.reshape(2 * block, span_count), span)
+        size = x.shape[1] * width
+        w = span_product(x.reshape(2 * size, span_count), span)
         halfway = (
-            w[:block, :span_count] - w[block:, span_count:],
-            w[:block, span_count:] + w[block:, :span_count],
+            w[:size, :span_count] - w[size:, span_count:],
+            w[:size, span_count:] + w[size:, :span_count],
         )
-        for g in range(chunks):
+        for g in range(low, high):
             for part in range(2):
                 for group in range(groups):
                     lanes = slice(LANES * group, LANES * (group + 1))
-                    start = width * QUAD * g
+                    start = width * QUAD * (g - low)
                     parts = [halfway[part][start + width * y : start + width * (y + 1), lanes] for y in range(QUAD)]
                     for i, tile in enumerate(swap_groups(parts)):
                         out1[h, g, QUAD * group + i, part] = tile
@@ -292,28 +284,47 @@
             for g in range(1, chunks):
                 first(0, g).start()
 
+    def every_tile_row(action):
+        size = stream_len // HALVES
+
+        def body(index, carry):
+            action(pl.ds(pl.multiple_of(index * size, size), size))
+            return carry
+
+        lax.fori_loop(0, HALVES, body, 0)
+
+    def return_half(h, g):
+        y = split_product(forward, slice(h * block * 4, (h + 1) * block * 4), slice(None), damped.at[g])
+        out2[h, g] = y.reshape(count, 2, width, LANES)
+
     def physical(again):
+        early, late = slice(0, stream_len // HALVES), slice(stream_len // HALVES, stream_len)
         first(1, 0).finish()
         for g in range(1, chunks):
             first(1, g).start()
         for g in range(chunks):
-            for h in range(HALVES):
-                first(h, g).arrive()
-                fill_pair(pair, slice(h * block * 4, (h + 1) * block * 4), in1[h, g].reshape(-1, LANES))
+            first(0, g).arrive()
+            fill_pair(pair, early, in1[0, g].reshape(-1, LANES))
+
+            def begin(at):
+                partial[g, at, :] = split_product(inverse, at, early, pair.at[early])
+
+            every_tile_row(begin)
+        for g in range(chunks):
+            first(1, g).arrive()
+            fill_pair(pair, late, in1[1, g].reshape(-1, LANES))
             if again:
                 second(1, g).finish()
 
-            def damp(index, at, y):
-                fill_pair(damped, at, y * drag[g, at, :])
-
-            stream_product(inverse, pair, damp)
-
-            def keep(index, at, y):
-                out2[index, g] = y.reshape(count, 2, width, LANES)
-
-            stream_product(forward, damped, keep)
+            def damp(at):
+                y = partial[g, at, :] + split_product(inverse, at, late, pair.at[late])
+                fill_pair(damped.at[g], at, y * drag[g, at, :])
+
+            every_tile_row(damp)
+            return_half(0, g)
             second(0, g).start()
         for g in range(chunks):
+            return_half(1, g)
             first(0, g).finish()
             if g:
                 first(1, g).finish()
@@ -324,27 +335,32 @@
         for g in range(1, chunks):
             second(0, g).finish()
 
-    def collect(h):
-        for g in range(chunks):
-            second(h, g).arrive()
-
-        @pl.when(h == 0)
-        def _():
-            for g in range(1, chunks):
-                second(1, g).start()
-
+    def collect(h, low=0, high=chunks):
         parts = []
         for part in range(2):
-            for g in range(chunks):
+            for g in range(low, high):
                 columns = []
                 for group in range(groups):
                     pieces = [in2[h, g, QUAD * group + i, part] for i in range(QUAD)]
                     columns.append(jnp.concatenate(swap_groups(pieces), axis=0))
                 parts.append(jnp.concatenate(columns, axis=1))
         w = span_product(jnp.concatenate(parts, axis=0), span)
-        shape = (rows, width, span_count)
-        drag_term[0] = (w[:block, :span_count] + w[block:, span_count:]).reshape(shape)
-        drag_term[1] = (w[block:, :span_count] - w[:block, span_count:]).reshape(shape)
+        size = w.shape[0] // 2
+        shape = (size // width, width, span_count)
+        lines = slice(QUAD * low, QUAD * high)
+        drag_term[0, lines] = (w[:size, :span_count] + w[size:, span_count:]).reshape(shape)
+        drag_term[1, lines] = (w[size:, :span_count] - w[:size, span_count:]).reshape(shape)
+
+    def receive(h):
+        for g in range(chunks):
+            second(h, g).arrive()
+
+        @pl.when(h == 0)
+        def _():
+            for g in range(1, chunks):
+                second(1, g).start()
+
+        collect(h)
 
     def spread(h, forced):
         def body(at, sub, column):
@@ -514,6 +530,10 @@
         every_tile(body)
 
     def start_reply():
+        reach_up = [has_above * lift[slab * (rows - 1)]] + [lift[slab * rows + y] for y in range(rows - 1)]
+        reach_down = [lift[slab * rows + y] for y in range(1, rows)] + [has_below * lift[rows]]
+        lift_slope = [0.5 * (down - up) for up, down in zip(reach_up, reach_down)]
+
         def body(h):
             def tile(at, sub, column):
                 for i in range(rows):
@@ -543,14 +563,14 @@
 
         every_half(body)
 
-    def close_wall(h):
+    def close_wall(h, g):
         def body(at, sub, column):
             kx, _ = waves(h, sub, column)
             kx = kx * mode_weight(h, sub)
             for p in range(2):
                 sign = 1.0 if p == 0 else -1.0
                 total = wall[(p, h) + at]
-                for y in range(rows):
+                for y in range(QUAD * g, QUAD * (g + 1)):
                     value = source[(p, y, h) + at] + sign * (kx * drag_term[(1 - p, y) + at])
                     total = total + reply[(y, h) + at] * value
                 wall[(p, h) + at] = total
@@ -572,11 +592,12 @@
 
     loads["stream"].wait()
     loads["span"].wait()
-    for name in ("control", "forward", "rest", "schur", "drag", "inverse"):
+    for name in ("lift", "control", "forward", "rest", "schur", "drag", "inverse"):
         loads[name].start()
-    pack_first(0, True)
-    pl.semaphore_wait(barrier, count)
     for g in range(chunks):
+        pack_first(0, True, g, g + 1)
+        if g == 0:
+            pl.semaphore_wait(barrier, count)
         first(0, g).start()
     pack_first(1, True)
     first(1, 0).start()
@@ -587,18 +608,20 @@
     blank = jnp.zeros((LANES - lines.shape[0], stream_len), jnp.float32)
     fill_pair(pair, slice(None), jnp.concatenate([lines, blank], axis=0).T)
 
-    def pack(index, at, y):
-        y = y.reshape(count, QUAD, SUBLANES, LANES)
-        moved = y[:, 0]
-        for j in range(1, QUAD):
-            moved = moved + pltpu.roll(y[:, j], j * LANES // QUAD, 2)
-        outc[index] = moved
-
-    stream_product(forward, pair, pack)
-    every_half(lambda h: third(h).start())
+    half = forward.shape[1] // HALVES
+    places = pl.ds(pl.multiple_of(slab * half, half), half)
+    y = mxu(forward[0, places, :], pair[...])
+    y = y[:, :LANES] + (y[:, LANES:] + mxu(forward[1, places, :], pair[:, :LANES]))
+    y = y.reshape(count, QUAD, SUBLANES, LANES)
+    moved = y[:, 0]
+    for j in range(1, QUAD):
+        moved = moved + pltpu.roll(y[:, j], j * LANES // QUAD, 2)
+    outc[...] = moved
+    third.start()
     loads["rest"].wait()
     every_half(start_halos)
     loads["schur"].wait()
+    loads["lift"].wait()
     corner_copy.start()
     start_reply()
     loads["drag"].wait()
@@ -607,26 +630,26 @@
     loads["inverse"].wait()
     physical(False)
 
-    def control_half(h):
-        third(h).arrive()
-        columns = []
-        for group in range(groups):
-            pieces = [inc[h, QUAD * group + i] for i in range(QUAD)]
-            columns.append(jnp.concatenate(swap_groups(pieces), axis=0))
-        w = span_product(jnp.concatenate(columns, axis=1), span)
-        control_hat[0, h] = w[:width, :span_count] + w[width:, span_count:]
-        control_hat[1, h] = w[width:, :span_count] - w[:width, span_count:]
-        third(h).finish()
-
-    every_half(control_half)
+    third.arrive()
+    columns = []
+    for group in range(groups):
+        pieces = [inc[QUAD * group + i] for i in range(QUAD)]
+        columns.append(jnp.concatenate(swap_groups(pieces), axis=0))
+    w = span_product(jnp.concatenate(columns, axis=1), span)
+    control_hat[0, slab] = w[:width, :span_count] + w[width:, span_count:]
+    control_hat[1, slab] = w[width:, :span_count] - w[:width, span_count:]
+    third.finish()
+    control_copy.start()
     corner_copy.wait_recv()
     corner_copy.wait_send()
     finish_reply()
+    control_copy.wait_recv()
+    control_copy.wait_send()
     spread_all(True)
     send_rest()
 
     def step(h):
-        collect(h)
+        receive(h)
         begin_solve(h)
         swap_rims(h, 0)
         finish_solve(h, fields)
@@ -639,7 +662,7 @@
     send_rest()
 
     def turn(h):
-        collect(h)
+        receive(h)
         begin_solve(h)
         swap_rims(h, 0)
         finish_and_reverse(h)
@@ -654,8 +677,21 @@
     send_rest()
 
     def close(h):
-        collect(h)
-        close_wall(h)
+        for g in range(chunks):
+            second(h, g).arrive()
+            if g == chunks - 1:
+
+                @pl.when(h == 0)
+                def _():
+                    for later in range(1, chunks):
+                        second(1, later).start()
+
+                @pl.when(h == 1)
+                def _():
+                    fourth(0).start()
+
+            collect(h, g, g + 1)
+            close_wall(h, g)
         w = span_product(wall[:, h].reshape(2 * width, span_count), span)
         halfway = (
             w[:width, :span_count] - w[width:, span_count:],
@@ -666,7 +702,6 @@
             pieces = [half[at : at + SUBLANES, lanes] for half in halfway for at in range(0, width, SUBLANES)]
             for i, tile in enumerate(swap_groups(pieces)):
                 outp[h, QUAD * group + i] = tile
-        fourth(h).start()
 
     def open_plane(h):
         fourth(h).arrive()
@@ -684,6 +719,7 @@
         return y[:, :LANES] + (y[:, LANES:] + mxu(inverse[1, places, terms], pair[terms, :LANES]))
 
     every_half(close)
+    fourth(1).start()
     share[...] = open_plane(0)
     gradient[...] = (share[...] + open_plane(1)).T[: gradient.shape[0]]
     for h in range(HALVES):
@@ -693,7 +729,6 @@
 
 
 VMEM = pl.BlockSpec(memory_space=pltpu.VMEM)
-SMEM = pl.BlockSpec(memory_space=pltpu.SMEM)
 FAR = pl.BlockSpec(memory_space=pltpu.HBM)
 
 
@@ -718,26 +753,26 @@
         return pltpu.VMEM(shape, jnp.float32)
 
     pairs = pltpu.VMEM((stream_len, 2 * LANES), jnp.bfloat16)
-    scratch = [buffer(*state.shape)] * 2 + [buffer(*plane), buffer(*half_plane), buffer(*half_plane)]
+    scratch = [pltpu.SMEM(lift_profile.shape, jnp.float32)] + [buffer(*state.shape)] * 2 + [buffer(*plane), buffer(*half_plane), buffer(*half_plane)]
     scratch += [buffer(*schur.shape), buffer(*drag_rate.shape), buffer(chunks, stream_len, LANES)]
     scratch += [buffer(*wall_control.shape), buffer(*line)]
     scratch += [pltpu.VMEM(table.shape, jnp.bfloat16) for table in (span, inverse, forward)]
-    scratch += [buffer(*box)] * 4 + [pairs] * 2 + [buffer(*thin)] * 4
+    scratch += [buffer(*box)] * 4 + [pairs, pltpu.VMEM((chunks, stream_len, 2 * LANES), jnp.bfloat16), buffer(chunks, stream_len, LANES)] + [buffer(*thin[1:])] * 2 + [buffer(*thin)] * 2
     scratch += [buffer(*line), buffer(HALVES, 2, 2, width, span_count), buffer(*line), buffer(*line)]
     scratch += [buffer(2, HALVES, 2, 2, width, span_count), buffer(2, HALVES, width, span_count), buffer(*line)]
     scratch += [buffer(rows, HALVES, width, span_count), buffer(HALVES, width, span_count)]
     scratch += [buffer(*thin), buffer(stream_len // 2, LANES)]
-    scratch += [pltpu.SemaphoreType.DMA((8,))]
+    scratch += [pltpu.SemaphoreType.DMA((9,))]
     scratch += [pltpu.SemaphoreType.DMA((2, HALVES, chunks))] * 2
     scratch += [pltpu.SemaphoreType.DMA((2, HALVES))] * 2
-    scratch += [pltpu.SemaphoreType.DMA((6 * HALVES + 2,))] * 2
+    scratch += [pltpu.SemaphoreType.DMA((6 * HALVES + 3,))] * 2
     final, gradient = pl.pallas_call(
         functools.partial(fused_kernel, count, stream_len),
         out_shape=[
             pltpu.VMEM(state.shape, jnp.float32),
             pltpu.VMEM((narrow, stream_len // 2), jnp.float32),
         ],
-        in_specs=[SMEM] + [FAR] * 7,
+        in_specs=[FAR] * 8,
         out_specs=[VMEM, VMEM],
         scratch_shapes=scratch,
         compiler_params=pltpu.CompilerParams(

time: 162 us -> 157 us (0.969)
  Pallas kernels: 159 us -> 154 us
    pallas_call x1, Pallas kernels: 159 us -> 154 us  [fused_call(): pl.pallas_call(functools.partial(fused_kernel, count, stream_len), out_sh...]
where the time goes in v2:
time: 157 us
  Pallas kernels  154 us (98%)
  local copies, waits for them, and re-layouts  2.3 us (1%)
    pallas_call x1, Pallas kernels, fused_call(): pl.pallas_call(functools.partial(fused_kernel, count, stream_len), out_sh...  154 us

profile of v2, /device:TPU:0, one launch (start us, length us, event | category | flops | bytes accessed | tf_op | source)
XLA Modules:
  0.0 156.9 jit_solution(10728591471926969967)
XLA Ops:
  0.6 154.0 %shard_map.95 = (f32[3,2,8,2,16,512]{5,4,3,2,1,0:T(8,128)S(1)}, f32[32,512]{1,0:T(8,128)S(1)}) custom-call(f32[16]{0:T(128)} %refs_0_.1, f32[3,2,8,2,16,512]{5,4,3,2,1,0:T(8,128)} %bitcast.5, f32[8,32,1024]{2,1,0:T(8,128)} %refs_2_.1, f32[32,1024]{1,0:T(8,128)} %refs_3_.1, f32[8,8,2,16,512]{4,3,2,1,0:T(8,128)} %bitcast.4, ...), custom_call_target="tpu_custom_call" | custom-call | flops 60000002048 | bytes 32000000 | tf_op jit(solution)/shard_map/pallas_call | solution.py:769
  154.7 1.7 %copy.12 = f32[3,2,8,32,512]{4,3,2,1,0:T(8,128)} copy(f32[3,2,8,32,512]{4,3,2,1,0:T(8,128)S(1)} %bitcast.3) | data formatting | bytes 6291456
  156.3 0.6 copy.13

commit v3 on v2

--- a/solution.py
+++ b/solution.py
@@ -299,7 +299,6 @@
 
     def physical(again):
         early, late = slice(0, stream_len // HALVES), slice(stream_len // HALVES, stream_len)
-        first(1, 0).finish()
         for g in range(1, chunks):
             first(1, g).start()
         for g in range(chunks):
@@ -326,8 +325,7 @@
         for g in range(chunks):
             return_half(1, g)
             first(0, g).finish()
-            if g:
-                first(1, g).finish()
+            first(1, g).finish()
 
     def send_rest():
         second(0, 0).finish()

time: 157 us -> 156 us (level)
  no operation moved by 1% of the time
where the time goes in v3:
time: 156 us
  Pallas kernels  153 us (98%)
  local copies, waits for them, and re-layouts  2.3 us (1%)
    pallas_call x1, Pallas kernels, fused_call(): pl.pallas_call(functools.partial(fused_kernel, count, stream_len), out_sh...  153 us

profile of v3, /device:TPU:0, one launch (start us, length us, event | category | flops | bytes accessed | tf_op | source)
XLA Modules:
  0.0 156.2 jit_solution(9310262887477689408)
XLA Ops:
  0.6 153.3 %shard_map.95 = (f32[3,2,8,2,16,512]{5,4,3,2,1,0:T(8,128)S(1)}, f32[32,512]{1,0:T(8,128)S(1)}) custom-call(f32[16]{0:T(128)} %refs_0_.1, f32[3,2,8,2,16,512]{5,4,3,2,1,0:T(8,128)} %bitcast.5, f32[8,32,1024]{2,1,0:T(8,128)} %refs_2_.1, f32[32,1024]{1,0:T(8,128)} %refs_3_.1, f32[8,8,2,16,512]{4,3,2,1,0:T(8,128)} %bitcast.4, ...), custom_call_target="tpu_custom_call" | custom-call | flops 60000002048 | bytes 32000000 | tf_op jit(solution)/shard_map/pallas_call | solution.py:767
  153.9 1.7 %copy.12 = f32[3,2,8,32,512]{4,3,2,1,0:T(8,128)} copy(f32[3,2,8,32,512]{4,3,2,1,0:T(8,128)S(1)} %bitcast.3) | data formatting | bytes 6291456
  155.6 0.6 copy.13

commit v4 on v3

--- a/solution.py
+++ b/solution.py
@@ -328,9 +328,8 @@
             first(1, g).finish()
 
     def send_rest():
-        second(0, 0).finish()
         second(1, 0).start()
-        for g in range(1, chunks):
+        for g in range(chunks):
             second(0, g).finish()
 
     def collect(h, low=0, high=chunks):

time: 156 us -> 156 us (level)
  no operation moved by 1% of the time
where the time goes in v4:
time: 156 us
  Pallas kernels  153 us (98%)
  local copies, waits for them, and re-layouts  2.3 us (1%)
    pallas_call x1, Pallas kernels, fused_call(): pl.pallas_call(functools.partial(fused_kernel, count, stream_len), out_sh...  153 us

profile of v4, /device:TPU:0, one launch (start us, length us, event | category | flops | bytes accessed | tf_op | source)
XLA Modules:
  0.0 156.2 jit_solution(6402271417245756091)
XLA Ops:
  0.6 153.2 %shard_map.95 = (f32[3,2,8,2,16,512]{5,4,3,2,1,0:T(8,128)S(1)}, f32[32,512]{1,0:T(8,128)S(1)}) custom-call(f32[16]{0:T(128)} %refs_0_.1, f32[3,2,8,2,16,512]{5,4,3,2,1,0:T(8,128)} %bitcast.5, f32[8,32,1024]{2,1,0:T(8,128)} %refs_2_.1, f32[32,1024]{1,0:T(8,128)} %refs_3_.1, f32[8,8,2,16,512]{4,3,2,1,0:T(8,128)} %bitcast.4, ...), custom_call_target="tpu_custom_call" | custom-call | flops 60000002048 | bytes 32000000 | tf_op jit(solution)/shard_map/pallas_call | solution.py:766
  153.9 1.7 %copy.12 = f32[3,2,8,32,512]{4,3,2,1,0:T(8,128)} copy(f32[3,2,8,32,512]{4,3,2,1,0:T(8,128)S(1)} %bitcast.3) | data formatting | bytes 6291456
  155.5 0.6 copy.13
